TPU v7x, 32 devices: a whole 2x2x4 slice. The times are simulated.
32 devices in a mesh: nest: 2 (over core), row: 4 (over y, x), col: 4 (over z).
Axes of the slice: x: 2, y: 2, z: 4, core: 2. Of those that a mesh axis runs over, the one named last changes fastest.
Arguments:
- strips: float32 [2, 3, 4, 16, 24, 1536], P('nest', None, None, ('row', 'col')), may hold values from -1.5 to 2, as said below
- anchor: int32 [2, 2], replicated, may hold values from 1 to 127
- wet_mask: int32 [2, 512, 512], P('nest', 'row', 'col'), may hold values 0 or 1
- bathy_index: int32 [2, 512, 512], P('nest', 'row', 'col'), may hold values from 0 to 15
- bed_levels: float32 [16], replicated, may hold values from 0 to 1.5
- coarse: float32 [3, 1024, 512], P(None, ('nest', 'row'), 'col'), may hold values from -6 to 6
Outputs:
- fine_fields: float32 [2, 3, 1536, 1536], P('nest', None, 'row', 'col')
- coarse_next: float32 [3, 1024, 512], P(None, ('nest', 'row'), 'col')
Inputs may be any that keep to these rules, and one draw needn't show every extreme that they name: `strips`: plane 0 of the second dimension is the water depth, within 0.5 to 2; planes 1 and 2 are momenta within -1.5 to 1.5. anchor[n] holds the row and then the column offset of nest n's first coarse cell within its block of coarse rows.
All inputs are finite; a program needn't handle non-finite values. No bound on the sum of `wet_mask` on one device may be relied on, other than what follows from the above.
Results may differ from a plain program's by a relative error of at most 0.0003.
Values sent between devices are 32-bit elements; how exact they have to be, the bound alone decides.
No kernel may reach another device: no remote copies, remote signals or barrier semaphores. Data moves between devices by JAX's collectives and lax.ppermute only.
A program may use at most 128 MiB of HBM per device.

v0:
```python
import jax
import jax.numpy as jnp
from jax import lax
from jax.sharding import PartitionSpec as P

gravity = 1.0
courant = 0.2


def padded_2(cells, sides, width):
    for axis, dim in sides:
        count = lax.axis_size(axis)
        ends = count - 1
        head = lax.slice_in_dim(cells, 0, width, axis=dim)
        tail = lax.slice_in_dim(cells, cells.shape[dim] - width, cells.shape[dim], axis=dim)
        cells = jnp.concatenate(
            [
                lax.ppermute(tail, axis, [(i, (i + 1) % count) for i in range(ends)]),
                cells,
                lax.ppermute(head, axis, [((i + 1) % count, i) for i in range(ends)]),
            ],
            axis=dim,
        )
    return cells


def passed_along(block, axis, distance):
    devices = range(lax.axis_size(axis))
    route = [(i - distance, i) for i in devices if i - distance in devices]
    return lax.ppermute(block, axis, route)


def advance(padded, bed_pad, wet_pad):
    depth_now = padded[0]
    flow_u = padded[1]
    flow_v = padded[2]
    depth_safe = jnp.where(wet_pad > 0.5, depth_now, 1.0)
    speed_u = flow_u / depth_safe
    speed_v = flow_v / depth_safe
    celerity = jnp.sqrt(gravity * depth_safe)
    pressure = 0.5 * gravity * depth_safe * depth_safe
    fluxes_x = (flow_u, flow_u * speed_u + pressure, flow_v * speed_u)
    fluxes_y = (flow_v, flow_u * speed_v, flow_v * speed_v + pressure)
    reach_x = jnp.abs(speed_u) + celerity
    reach_y = jnp.abs(speed_v) + celerity
    open_x = wet_pad[1:-1, :-1] * wet_pad[1:-1, 1:]
    open_y = wet_pad[:-1, 1:-1] * wet_pad[1:, 1:-1]
    bound_x = jnp.maximum(reach_x[1:-1, :-1], reach_x[1:-1, 1:])
    bound_y = jnp.maximum(reach_y[:-1, 1:-1], reach_y[1:, 1:-1])
    slope_x = (bed_pad[1:-1, 1:] - bed_pad[1:-1, :-1]) * open_x
    slope_y = (bed_pad[1:, 1:-1] - bed_pad[:-1, 1:-1]) * open_y
    centre = depth_now[1:-1, 1:-1]
    sources = (
        None,
        -0.5 * gravity * centre * (slope_x[:, 1:] + slope_x[:, :-1]),
        -0.5 * gravity * centre * (slope_y[1:] + slope_y[:-1]),
    )
    results = []
    for plane in range(3):
        state = padded[plane]
        flux_col = fluxes_x[plane]
        flux_row = fluxes_y[plane]
        face_x = (
            0.5 * (flux_col[1:-1, :-1] + flux_col[1:-1, 1:])
            - 0.5 * bound_x * (state[1:-1, 1:] - state[1:-1, :-1])
        ) * open_x
        face_y = (
            0.5 * (flux_row[:-1, 1:-1] + flux_row[1:, 1:-1])
            - 0.5 * bound_y * (state[1:, 1:-1] - state[:-1, 1:-1])
        ) * open_y
        value = (
            state[1:-1, 1:-1]
            - courant * (face_x[:, 1:] - face_x[:, :-1])
            - courant * (face_y[1:] - face_y[:-1])
        )
        if plane > 0:
            value = value + courant * sources[plane]
        results.append(value)
    return jnp.stack(results)


def expand(cells):
    return jnp.repeat(jnp.repeat(cells, 3, axis=-2), 3, axis=-1)


def lookup(classes, levels):
    ladder = jnp.arange(levels.shape[0], dtype=jnp.int32)
    matches = classes[None] == ladder[:, None, None]
    return jnp.sum(jnp.where(matches, levels[:, None, None], 0.0), axis=0)


def restrict(updated):
    planes, row_count, col_count = updated.shape
    return updated.reshape(planes, row_count // 3, 3, col_count // 3, 3).sum(axis=(2, 4)) / 9.0


def local(strips, anchor, wet_mask, bathy_index, bed_levels, coarse):
    tile_blocks = strips.shape[2]
    band_rows = strips.shape[4]
    full_cols = strips.shape[5]
    columns = lax.axis_size("col")
    tile_cols = full_cols // columns
    layered = (
        strips[0, :, :, 0]
        .reshape(3, tile_blocks, band_rows, columns, tile_cols)
        .transpose(0, 1, 3, 2, 4)
    )
    flattened = layered.reshape(3, tile_blocks * columns, band_rows, tile_cols)
    arrived = lax.all_to_all(flattened, ("row", "col"), split_axis=1, concat_axis=1, tiled=True)
    fields = arrived.reshape(3, tile_blocks * columns * band_rows, tile_cols)
    classes = bathy_index[0]
    wet_cells = wet_mask[0]
    bed_fine = expand(lookup(classes, bed_levels))
    wetness = expand(wet_cells.astype(jnp.float32))
    stacked = jnp.concatenate([fields, bed_fine[None], wetness[None]], axis=0)
    padded_all = padded_2(stacked, (("row", 1), ("col", 2)), 1)
    padded = padded_all[:3]
    bed_pad = padded_all[3]
    wet_pad = padded_all[4]
    updated = advance(padded, bed_pad, wet_pad)
    restricted = restrict(updated)
    coarse_rows = restricted.shape[1]
    coarse_cols = restricted.shape[2]
    contribution = jnp.concatenate(
        [restricted, jnp.ones((1, coarse_rows, coarse_cols), jnp.float32)], axis=0
    )
    nest_index = lax.axis_index("nest")
    corner = lax.dynamic_index_in_dim(anchor, nest_index, 0, keepdims=False)
    canvas = lax.dynamic_update_slice(
        jnp.zeros((4, 2 * coarse_rows, 2 * coarse_cols), jnp.float32),
        contribution,
        (jnp.int32(0), corner[0], corner[1]),
    )
    spilled = passed_along(canvas[:, :, coarse_cols:], "col", 1)
    merged = canvas[:, :, :coarse_cols] + spilled
    lowered = passed_along(merged[:, coarse_rows:], ("nest", "row"), 1)
    received_sum = merged[:, :coarse_rows] + lowered
    coarse_next = (coarse + received_sum[:3]) / (1.0 + received_sum[3])
    return (updated[None], coarse_next)


def solution(mesh):
    return jax.shard_map(
        local,
        mesh=mesh,
        in_specs=(
            P("nest", None, None, ("row", "col"), None, None),
            P(),
            P("nest", "row", "col"),
            P("nest", "row", "col"),
            P(),
            P(None, ("nest", "row"), "col"),
        ),
        out_specs=(P("nest", None, "row", "col"), P(None, ("nest", "row"), "col")),
        check_vma=False,
    )
```

profile of v0, /device:TPU:12, one launch (start us, length us, event | category | flops | bytes accessed | tf_op | source)
XLA Modules:
  0.0 250.1 jit_solution(6298156898916044480)
XLA Ops:
  0.6 1.9 reshape_squeeze.3
  2.6 1.3 copy.37
  3.9 7.3 %all-to-all-start = ((f32[3,16,24,384]{3,2,0,1:T(8,128)}), f32[3,16,24,384]{3,2,0,1:T(8,128)}, u32[]{:S(2)}, u32[]{:S(2)}) async-start(f32[3,16,24,384]{3,2,0,1:T(8,128)} %bitcast.1), calls=%async_computation | async-start | bytes 3538944 | tf_op jit(solution)/shard_map/all_to_all | solution.py:109
  11.4 0.1 copy.40
  11.5 0.1 broadcast_in_dim.43
  11.6 0.3 broadcast_in_dim_reshape.7
  11.9 0.2 copy.42
  12.2 0.2 select_reduce_fusion
  12.6 0.1 broadcast_in_dim.41
  12.8 0.3 broadcast_in_dim_reshape.6
  13.1 0.2 copy.41
  13.3 36.6 %all-to-all-done = f32[3,16,24,384]{3,2,0,1:T(8,128)} async-done(((f32[3,16,24,384]{3,2,0,1:T(8,128)}), f32[3,16,24,384]{3,2,0,1:T(8,128)}, u32[]{:S(2)}, u32[]{:S(2)}) %all-to-all-start) | async-done | bytes 1769504 | tf_op jit(solution)/shard_map/all_to_all | solution.py:109
  50.0 1.6 copy.38
  51.6 3.1 %collective-permute-start.1 = (f32[5,1,384]{2,1,0:T(1,128)S(1)}, f32[5,1,384]{2,1,0:T(1,128)S(1)}, u32[]{:S(2)}, u32[]{:S(2)}) collective-permute-start(f32[5,1,384]{2,1,0:T(1,128)S(1)} %get-tuple-element.23), channel_id=1, source_target_pairs={{4,0},{8,4},{12,8},{5,1},{9,5},{13,9},{6,2},{10,6},{14,10},{7,3},{... | collective-permute-start | bytes 23048 | tf_op jit(solution)/shard_map/ppermute | solution.py:20
  54.7 2.8 %collective-permute-start = (f32[5,1,384]{2,1,0:T(1,128)S(1)}, f32[5,1,384]{2,1,0:T(1,128)S(1)}, u32[]{:S(2)}, u32[]{:S(2)}) collective-permute-start(f32[5,1,384]{2,1,0:T(1,128)S(1)} %get-tuple-element.22), channel_id=1, source_target_pairs={{0,4},{4,8},{8,12},{1,5},{5,9},{9,13},{2,6},{6,10},{10,14},{3,7},{... | collective-permute-start | bytes 23048 | tf_op jit(solution)/shard_map/ppermute | solution.py:18
  57.5 3.6 %collective-permute-done = f32[5,1,384]{2,1,0:T(1,128)S(1)} collective-permute-done((f32[5,1,384]{2,1,0:T(1,128)S(1)}, f32[5,1,384]{2,1,0:T(1,128)S(1)}, u32[]{:S(2)}, u32[]{:S(2)}) %collective-permute-start) | collective-permute-done | bytes 7712 | tf_op jit(solution)/shard_map/ppermute | solution.py:18
  61.1 1.6 pad_maximum_fusion.5
  62.7 1.6 copy.44
  64.3 4.7 %collective-permute-start.3 = (f32[5,386,1]{1,2,0:T(1,128)S(1)}, f32[5,386,1]{1,2,0:T(1,128)S(1)}, u32[]{:S(2)}, u32[]{:S(2)}) collective-permute-start(f32[5,386,1]{1,2,0:T(1,128)S(1)} %copy.44), channel_id=1, source_target_pairs={{1,0},{2,1},{3,2},{5,4},{6,5},{7,6},{9,8},{10,9},{11,10},{13,12},{... | collective-permute-start | bytes 23168 | tf_op jit(solution)/shard_map/ppermute | solution.py:20
  69.0 1.6 copy.43
  70.7 2.1 collective-permute-start.2
  72.8 0.6 fusion.48
  77.2 1.3 copy.46
  78.6 1.4 copy.45
  79.9 5.5 %pad_maximum_fusion = f32[5,386,386]{2,1,0:T(8,128)S(1)} fusion(f32[5,386,1]{2,1,0:T(8,128)} %copy.46, f32[5,1,384]{2,1,0:T(1,128)S(1)} %collective-permute-done.1, f32[1,384,384]{2,1,0:T(8,128)S(1)} %copy.42, f32[1,384,384]{2,1,0:T(8,128)S(1)} %copy.41, f32[3,384,384]{2,1,0:T(8,128)S(1)} %bitcast.64, f32[5,1,384]{2,1,0:T(1,128)S(1)} %collective-permute-done, ...), kind=kLoop, calls=%fused_computation | loop fusion | flops 4469880 | bytes 5959840 | tf_op jit(solution)/shard_map/concatenate | solution.py:16
  85.4 0.5 slice_bitcast_fusion.3
  85.9 0.3 multiply_add_fusion.1
  86.2 0.5 fusion.44
  86.7 2.2 fusion.22
  88.9 1.9 fusion.10
  90.8 2.8 %fusion.18 = (f32[385,384]{1,0:T(8,128)}, f32[385,384]{1,0:T(8,128)S(1)}, f32[385,384]{1,0:T(8,128)S(1)}) fusion(f32[385,384]{1,0:T(8,128)S(1)} %get-tuple-element.7, f32[386,386]{1,0:T(8,128)S(1)} %get-tuple-element.15, f32[386,386]{1,0:T(8,128)S(1)} %get-tuple-element.10, f32[386,386]{1,0:T(8,128)S(1)} %get-tuple-element.14, ...), kind=kLoop, calls=%fused_computation.49 | loop fusion | flops 2365440 | bytes 9461760 | tf_op jit(solution)/shard_map/mul | solution.py:67
  93.6 2.7 %fusion.7 = (f32[384,385]{1,0:T(8,128)}, f32[384,385]{1,0:T(8,128)S(1)}, f32[384,385]{1,0:T(8,128)}) fusion(f32[384,385]{1,0:T(8,128)S(1)} %get-tuple-element.5, f32[386,386]{1,0:T(8,128)S(1)} %get-tuple-element.8, f32[386,386]{1,0:T(8,128)S(1)} %get-tuple-element.15, f32[386,386]{1,0:T(8,128)S(1)} %get-tuple-element.13, ...), kind=kLoop, calls=%fused_computation.32 | loop fusion | flops 2365440 | bytes 9461760 | tf_op jit(solution)/shard_map/mul | solution.py:63
  96.3 0.6 fusion.26
  96.9 25.2 %stack.26 = f32[1,128,3,128,3]{4,3,2,1,0:T(8,128)} reshape(f32[384,384]{1,0:T(8,128)S(1)} %fusion.26) | data formatting | bytes 1179648 | tf_op jit(solution)/shard_map/stack | solution.py:79
  122.1 15.5 %copy.49 = f32[1,128,3,128,3]{3,1,4,2,0:T(8,128)} copy(f32[1,128,3,128,3]{4,3,2,1,0:T(8,128)} %stack.26) | data formatting | bytes 1179648 | tf_op jit(solution)/shard_map/stack | solution.py:79
  137.6 3.8 %fusion.39 = (f32[384,384]{1,0:T(8,128)S(1)}, f32[384,384]{1,0:T(8,128)S(1)}) fusion(f32[385,384]{1,0:T(8,128)} %get-tuple-element.6, f32[384,385]{1,0:T(8,128)} %get-tuple-element.4, f32[386,386]{1,0:T(8,128)S(1)} %get-tuple-element.19, f32[384,385]{1,0:T(8,128)} %get-tuple-element.30, f32[385,384]{1,0:T(8,128)} %get-tuple-element.26, ...), kind=kLoop, calls=%fused_computation.81 | loop fusion | flops 2506752 | bytes 8257536 | tf_op jit(solution)/shard_map/sub | solution.py:72
  141.4 25.2 %stack.25 = f32[1,128,3,128,3]{4,3,2,1,0:T(8,128)} reshape(f32[384,384]{1,0:T(8,128)S(1)} %get-tuple-element.29) | data formatting | bytes 1179648 | tf_op jit(solution)/shard_map/stack | solution.py:79
  166.6 14.8 %copy.48 = f32[1,128,3,128,3]{3,1,4,2,0:T(8,128)S(1)} copy(f32[1,128,3,128,3]{4,3,2,1,0:T(8,128)} %stack.25) | data formatting | bytes 1179648 | tf_op jit(solution)/shard_map/stack | solution.py:79
  181.4 25.2 %stack.24 = f32[1,128,3,128,3]{4,3,2,1,0:T(8,128)} reshape(f32[384,384]{1,0:T(8,128)S(1)} %get-tuple-element.28) | data formatting | bytes 1179648 | tf_op jit(solution)/shard_map/stack | solution.py:79
  206.6 15.5 %copy.47 = f32[1,128,3,128,3]{3,1,4,2,0:T(8,128)} copy(f32[1,128,3,128,3]{4,3,2,1,0:T(8,128)} %stack.24) | data formatting | bytes 1179648 | tf_op jit(solution)/shard_map/stack | solution.py:79
  222.1 1.2 maximum_reduce_fusion
  223.5 3.3 %dynamic_update_slice.3 = f32[4,256,256]{2,1,0:T(8,128)S(1)} dynamic-update-slice(f32[4,256,256]{2,1,0:T(8,128)S(1)} %broadcast_in_dim.46, f32[4,128,128]{2,1,0:T(8,128)S(1)} %concatenate.16, s32[]{:T(128)} %constant.5.clone.1, s32[]{:T(128)S(6)} %select_n.21, s32[]{:T(128)S(6)} %select_n.22) | dynamic-update-slice | bytes 524292 | tf_op jit(solution)/shard_map/dynamic_update_slice | solution.py:129
  226.8 2.6 %collective-permute-start.4 = (f32[4,256,128]{2,1,0:T(8,128)S(1)}, f32[4,256,128]{2,1,0:T(8,128)S(1)}, u32[]{:S(2)}, u32[]{:S(2)}) collective-permute-start(f32[4,256,128]{2,1,0:T(8,128)S(1)} %slice.343), channel_id=1, source_target_pairs={{0,1},{1,2},{2,3},{4,5},{5,6},{6,7},{8,9},{9,10},{10,11},{12,13},{... | collective-permute-start | bytes 1572872 | tf_op jit(solution)/shard_map/ppermute | solution.py:30
  229.4 10.6 %collective-permute-done.4 = f32[4,256,128]{2,1,0:T(8,128)S(1)} collective-permute-done((f32[4,256,128]{2,1,0:T(8,128)S(1)}, f32[4,256,128]{2,1,0:T(8,128)S(1)}, u32[]{:S(2)}, u32[]{:S(2)}) %collective-permute-start.4) | collective-permute-done | bytes 524320 | tf_op jit(solution)/shard_map/ppermute | solution.py:30
  240.2 2.5 collective-permute-start.5
  242.7 1.3 maximum_bitcast_fusion
  244.0 5.4 %collective-permute-done.5 = f32[4,128,128]{2,1,0:T(8,128)S(1)} collective-permute-done((f32[4,128,128]{2,1,0:T(8,128)S(1)}, f32[4,128,128]{2,1,0:T(8,128)S(1)}, u32[]{:S(2)}, u32[]{:S(2)}) %collective-permute-start.5) | collective-permute-done | bytes 262176 | tf_op jit(solution)/shard_map/ppermute | solution.py:30
  249.4 0.7 fusion.42
  (33 shorter events, 0.8 us)
Async XLA Ops:
  0.6 56.8 %copy-start = (s32[2,2]{1,0:T(2,128)S(1)}, s32[2,2]{1,0:T(2,128)}, u32[]{:S(2)}) copy-start(s32[2,2]{1,0:T(2,128)} %param.7) | copy-start | bytes 52
  2.5 8.6 %copy-start.4 = (s32[1,128,128]{2,1,0:T(8,128)S(1)}, s32[1,128,128]{2,1,0:T(8,128)}, u32[]{:S(2)}) copy-start(s32[1,128,128]{2,1,0:T(8,128)} %param.8) | copy-start | bytes 196612
  3.9 8.3 %copy-start.5 = (s32[1,128,128]{2,1,0:T(8,128)S(1)}, s32[1,128,128]{2,1,0:T(8,128)}, u32[]{:S(2)}) copy-start(s32[1,128,128]{2,1,0:T(8,128)} %param.9) | copy-start | bytes 196612
  3.9 8.3 %copy-start.6 = (f32[16]{0:T(128)S(1)}, f32[16]{0:T(128)}, u32[]{:S(2)}) copy-start(f32[16]{0:T(128)} %param.10) | copy-start | bytes 196
  3.9 46.1 %all-to-all-start = ((f32[3,16,24,384]{3,2,0,1:T(8,128)}), f32[3,16,24,384]{3,2,0,1:T(8,128)}, u32[]{:S(2)}, u32[]{:S(2)}) async-start(f32[3,16,24,384]{3,2,0,1:T(8,128)} %bitcast.1), calls=%async_computation | async-start | bytes 3538944 | tf_op jit(solution)/shard_map/all_to_all | solution.py:109
  51.6 5.9 %collective-permute-start.1 = (f32[5,1,384]{2,1,0:T(1,128)S(1)}, f32[5,1,384]{2,1,0:T(1,128)S(1)}, u32[]{:S(2)}, u32[]{:S(2)}) collective-permute-start(f32[5,1,384]{2,1,0:T(1,128)S(1)} %get-tuple-element.23), channel_id=1, source_target_pairs={{4,0},{8,4},{12,8},{5,1},{9,5},{13,9},{6,2},{10,6},{14,10},{7,3},{... | collective-permute-start | bytes 23048 | tf_op jit(solution)/shard_map/ppermute | solution.py:20
  54.7 6.4 %collective-permute-start = (f32[5,1,384]{2,1,0:T(1,128)S(1)}, f32[5,1,384]{2,1,0:T(1,128)S(1)}, u32[]{:S(2)}, u32[]{:S(2)}) collective-permute-start(f32[5,1,384]{2,1,0:T(1,128)S(1)} %get-tuple-element.22), channel_id=1, source_target_pairs={{0,4},{4,8},{8,12},{1,5},{5,9},{9,13},{2,6},{6,10},{10,14},{3,7},{... | collective-permute-start | bytes 23048 | tf_op jit(solution)/shard_map/ppermute | solution.py:18
  64.3 12.9 %collective-permute-start.3 = (f32[5,386,1]{1,2,0:T(1,128)S(1)}, f32[5,386,1]{1,2,0:T(1,128)S(1)}, u32[]{:S(2)}, u32[]{:S(2)}) collective-permute-start(f32[5,386,1]{1,2,0:T(1,128)S(1)} %copy.44), channel_id=1, source_target_pairs={{1,0},{2,1},{3,2},{5,4},{6,5},{7,6},{9,8},{10,9},{11,10},{13,12},{... | collective-permute-start | bytes 23168 | tf_op jit(solution)/shard_map/ppermute | solution.py:20
  70.7 7.9 %collective-permute-start.2 = (f32[5,386,1]{1,2,0:T(1,128)S(1)}, f32[5,386,1]{1,2,0:T(1,128)S(1)}, u32[]{:S(2)}, u32[]{:S(2)}) collective-permute-start(f32[5,386,1]{1,2,0:T(1,128)S(1)} %copy.43), channel_id=1, source_target_pairs={{0,1},{1,2},{2,3},{4,5},{5,6},{6,7},{8,9},{9,10},{10,11},{12,13},{... | collective-permute-start | bytes 23168 | tf_op jit(solution)/shard_map/ppermute | solution.py:18
  206.6 15.5 %copy-start.2 = (f32[1,128,3,128,3]{3,1,4,2,0:T(8,128)S(1)}, f32[1,128,3,128,3]{3,1,4,2,0:T(8,128)}, u32[]{:S(2)}) copy-start(f32[1,128,3,128,3]{3,1,4,2,0:T(8,128)} %copy.49) | copy-start | bytes 1769476
  223.5 26.6 %copy-start.1 = (s32[2,2]{1,0:T(2,128)S(1)}, s32[2,2]{1,0:T(2,128)}, u32[]{:S(2)}) copy-start(s32[2,2]{1,0:T(2,128)} %param.7) | copy-start | bytes 52
  226.8 22.6 %copy-start.3 = (f32[3,128,128]{2,1,0:T(8,128)S(1)}, f32[3,128,128]{2,1,0:T(8,128)}, u32[]{:S(2)}) copy-start(f32[3,128,128]{2,1,0:T(8,128)} %param.11) | copy-start | bytes 589828
  226.8 13.3 %collective-permute-start.4 = (f32[4,256,128]{2,1,0:T(8,128)S(1)}, f32[4,256,128]{2,1,0:T(8,128)S(1)}, u32[]{:S(2)}, u32[]{:S(2)}) collective-permute-start(f32[4,256,128]{2,1,0:T(8,128)S(1)} %slice.343), channel_id=1, source_target_pairs={{0,1},{1,2},{2,3},{4,5},{5,6},{6,7},{8,9},{9,10},{10,11},{12,13},{... | collective-permute-start | bytes 1572872 | tf_op jit(solution)/shard_map/ppermute | solution.py:30
  240.2 9.2 %collective-permute-start.5 = (f32[4,128,128]{2,1,0:T(8,128)S(1)}, f32[4,128,128]{2,1,0:T(8,128)S(1)}, u32[]{:S(2)}, u32[]{:S(2)}) collective-permute-start(f32[4,128,128]{2,1,0:T(8,128)S(1)} %slice.345), channel_id=1, source_target_pairs={{0,4},{4,8},{8,12},{12,16},{16,20},{20,24},{24,28},{1,5},{5,9},{9,... | collective-permute-start | bytes 786440 | tf_op jit(solution)/shard_map/ppermute | solution.py:30
where the time goes:
time: 251 us; the launch traced here: 250 us
  local copies, waits for them, and re-layouts  138 us (55%)
  waiting for transfers between devices  56.3 us (22%)
  other arithmetic  25.5 us (10%)
  starting transfers between devices  25.1 us (10%)
  between operations  4.88 us (2%)
    another operation x6, local copies, waits for them, and re-layouts, advance(): return jnp.stack(results)  121 us
    all_to_all x1, waiting for transfers between devices, local(): lax.all_to_all(flattened, ('row', 'col'), split_axis=1, concat_axis=1, ti...  36.6 us
    ppermute x2, waiting for transfers between devices, passed_along(): return lax.ppermute(block, axis, route)  16 us
    ppermute x2, starting transfers between devices, padded_2(): lax.ppermute(head, axis, [((i + 1) % count, i) for i in range(ends)])  7.81 us
    all_to_all x1, starting transfers between devices, local(): lax.all_to_all(flattened, ('row', 'col'), split_axis=1, concat_axis=1, ti...  7.3 us
    concatenate x1, other arithmetic, padded_2(): jnp.concatenate([lax.ppermute(tail, axis, [(i, (i + 1) % count) for i in...  5.51 us
    ppermute x2, starting transfers between devices, passed_along(): return lax.ppermute(block, axis, route)  5.1 us
  transfers between devices with their start and end apart: 7, of which 4 were waited for; matrix products, arithmetic and copies ran while one was open for 3% of the time, Pallas kernels for 0%

commit v1 on v0

--- a/solution.py
+++ b/solution.py
@@ -106,7 +106,10 @@
         .transpose(0, 1, 3, 2, 4)
     )
     flattened = layered.reshape(3, tile_blocks * columns, band_rows, tile_cols)
-    arrived = lax.all_to_all(flattened, ("row", "col"), split_axis=1, concat_axis=1, tiled=True)
+    n_dev = lax.axis_size(("row", "col"))
+    pieces = jnp.stack(jnp.split(flattened, n_dev, axis=1), axis=0)
+    pieces = lax.all_to_all(pieces, ("row", "col"), split_axis=0, concat_axis=0)
+    arrived = jnp.concatenate(pieces, axis=1)
     fields = arrived.reshape(3, tile_blocks * columns * band_rows, tile_cols)
     classes = bathy_index[0]
     wet_cells = wet_mask[0]

time: 251 us -> 260 us (1.036)
  local copies, waits for them, and re-layouts: 138 us -> 148 us
    unnamed x14 -> x29, local copies, waits for them, and re-layouts: 0.04 us -> 9.97 us
where the time goes in v1:
time: 260 us; the launch traced here: 259 us
  local copies, waits for them, and re-layouts  148 us (57%)
  waiting for transfers between devices  56.1 us (22%)
  other arithmetic  25.5 us (10%)
  starting transfers between devices  25 us (10%)
  between operations  4.89 us (2%)
    another operation x6, local copies, waits for them, and re-layouts, advance(): return jnp.stack(results)  121 us
    all_to_all x1, waiting for transfers between devices, local(): pieces = lax.all_to_all(pieces, ('row', 'col'), split_axis=0, concat_axis=0)  36.5 us
    ppermute x2, waiting for transfers between devices, passed_along(): return lax.ppermute(block, axis, route)  16 us
    unnamed x29, local copies, waits for them, and re-layouts  9.97 us
    ppermute x2, starting transfers between devices, padded_2(): lax.ppermute(head, axis, [((i + 1) % count, i) for i in range(ends)])  7.81 us
    all_to_all x1, starting transfers between devices, local(): pieces = lax.all_to_all(pieces, ('row', 'col'), split_axis=0, concat_axis=0)  7.3 us
    concatenate x1, other arithmetic, padded_2(): jnp.concatenate([lax.ppermute(tail, axis, [(i, (i + 1) % count) for i in...  5.51 us
  transfers between devices with their start and end apart: 7, of which 4 were waited for; matrix products, arithmetic and copies ran while one was open for 3% of the time, Pallas kernels for 0%

profile of v1, /device:TPU:12, one launch (start us, length us, event | category | flops | bytes accessed | tf_op | source)
XLA Modules:
  0.0 259.2 jit_solution(13016756139505442314)
XLA Ops:
  0.6 1.9 reshape_squeeze.3
  2.7 0.7 fusion.58
  3.3 0.7 fusion.57
  4.0 0.7 fusion.56
  4.6 0.7 fusion.55
  5.3 0.7 fusion.54
  5.9 0.7 fusion.53
  6.6 0.7 fusion.52
  7.2 0.7 fusion.51
  7.9 0.7 fusion.50
  8.5 0.7 fusion.49
  9.2 0.7 fusion.48
  9.8 0.7 fusion.47
  10.5 0.7 fusion.46
  11.8 0.7 fusion.44
  13.1 7.3 %all-to-all-start = ((f32[16,3,1,24,384]{4,3,1,2,0:T(8,128)}), f32[16,3,1,24,384]{4,3,1,2,0:T(8,128)}, u32[]{:S(2)}, u32[]{:S(2)}) async-start(f32[16,3,1,24,384]{4,3,1,2,0:T(8,128)} %fusion.43), calls=%async_computation | async-start | bytes 3538944 | tf_op jit(solution)/shard_map/all_to_all | solution.py:111
  22.7 36.5 %all-to-all-done = f32[16,3,1,24,384]{4,3,1,2,0:T(8,128)} async-done(((f32[16,3,1,24,384]{4,3,1,2,0:T(8,128)}), f32[16,3,1,24,384]{4,3,1,2,0:T(8,128)}, u32[]{:S(2)}, u32[]{:S(2)}) %all-to-all-start) | async-done | bytes 1769504 | tf_op jit(solution)/shard_map/all_to_all | solution.py:111
  59.2 1.6 copy.68
  60.8 3.1 %collective-permute-start.1 = (f32[5,1,384]{2,1,0:T(1,128)S(1)}, f32[5,1,384]{2,1,0:T(1,128)S(1)}, u32[]{:S(2)}, u32[]{:S(2)}) collective-permute-start(f32[5,1,384]{2,1,0:T(1,128)S(1)} %get-tuple-element.23), channel_id=1, source_target_pairs={{4,0},{8,4},{12,8},{5,1},{9,5},{13,9},{6,2},{10,6},{14,10},{7,3},{... | collective-permute-start | bytes 23048 | tf_op jit(solution)/shard_map/ppermute | solution.py:20
  63.9 2.8 %collective-permute-start = (f32[5,1,384]{2,1,0:T(1,128)S(1)}, f32[5,1,384]{2,1,0:T(1,128)S(1)}, u32[]{:S(2)}, u32[]{:S(2)}) collective-permute-start(f32[5,1,384]{2,1,0:T(1,128)S(1)} %get-tuple-element.22), channel_id=1, source_target_pairs={{0,4},{4,8},{8,12},{1,5},{5,9},{9,13},{2,6},{6,10},{10,14},{3,7},{... | collective-permute-start | bytes 23048 | tf_op jit(solution)/shard_map/ppermute | solution.py:18
  66.7 3.6 %collective-permute-done = f32[5,1,384]{2,1,0:T(1,128)S(1)} collective-permute-done((f32[5,1,384]{2,1,0:T(1,128)S(1)}, f32[5,1,384]{2,1,0:T(1,128)S(1)}, u32[]{:S(2)}, u32[]{:S(2)}) %collective-permute-start) | collective-permute-done | bytes 7712 | tf_op jit(solution)/shard_map/ppermute | solution.py:18
  70.3 1.6 pad_maximum_fusion.5
  71.9 1.6 copy.74
  73.5 4.7 %collective-permute-start.3 = (f32[5,386,1]{1,2,0:T(1,128)S(1)}, f32[5,386,1]{1,2,0:T(1,128)S(1)}, u32[]{:S(2)}, u32[]{:S(2)}) collective-permute-start(f32[5,386,1]{1,2,0:T(1,128)S(1)} %copy.74), channel_id=1, source_target_pairs={{1,0},{2,1},{3,2},{5,4},{6,5},{7,6},{9,8},{10,9},{11,10},{13,12},{... | collective-permute-start | bytes 23168 | tf_op jit(solution)/shard_map/ppermute | solution.py:20
  78.3 1.6 copy.73
  79.9 2.1 collective-permute-start.2
  86.5 1.3 copy.76
  87.8 1.4 copy.75
  89.2 5.5 %pad_maximum_fusion = f32[5,386,386]{2,1,0:T(8,128)S(1)} fusion(f32[5,386,1]{2,1,0:T(8,128)} %copy.76, f32[5,1,384]{2,1,0:T(1,128)S(1)} %collective-permute-done.1, f32[1,384,384]{2,1,0:T(8,128)S(1)} %copy.72, f32[1,384,384]{2,1,0:T(8,128)S(1)} %copy.71, f32[3,384,384]{2,1,0:T(8,128)S(1)} %bitcast.130, f32[5,1,384]{2,1,0:T(1,128)S(1)} %collective-permute-done, ...), kind=kLoop, calls=%fused_computation | loop fusion | flops 4469880 | bytes 5959840 | tf_op jit(solution)/shard_map/concatenate | solution.py:16
  96.0 2.2 fusion.22
  98.2 1.9 fusion.10
  100.1 2.8 %fusion.18 = (f32[385,384]{1,0:T(8,128)}, f32[385,384]{1,0:T(8,128)S(1)}, f32[385,384]{1,0:T(8,128)S(1)}) fusion(f32[385,384]{1,0:T(8,128)S(1)} %get-tuple-element.7, f32[386,386]{1,0:T(8,128)S(1)} %get-tuple-element.15, f32[386,386]{1,0:T(8,128)S(1)} %get-tuple-element.10, f32[386,386]{1,0:T(8,128)S(1)} %get-tuple-element.14, ...), kind=kLoop, calls=%fused_computation.49 | loop fusion | flops 2365440 | bytes 9461760 | tf_op jit(solution)/shard_map/mul | solution.py:67
  102.9 2.7 %fusion.7 = (f32[384,385]{1,0:T(8,128)}, f32[384,385]{1,0:T(8,128)S(1)}, f32[384,385]{1,0:T(8,128)}) fusion(f32[384,385]{1,0:T(8,128)S(1)} %get-tuple-element.5, f32[386,386]{1,0:T(8,128)S(1)} %get-tuple-element.8, f32[386,386]{1,0:T(8,128)S(1)} %get-tuple-element.15, f32[386,386]{1,0:T(8,128)S(1)} %get-tuple-element.13, ...), kind=kLoop, calls=%fused_computation.32 | loop fusion | flops 2365440 | bytes 9461760 | tf_op jit(solution)/shard_map/mul | solution.py:63
  106.2 25.2 %stack.94 = f32[1,128,3,128,3]{4,3,2,1,0:T(8,128)} reshape(f32[384,384]{1,0:T(8,128)S(1)} %fusion.26) | data formatting | bytes 1179648 | tf_op jit(solution)/shard_map/stack | solution.py:79
  131.4 15.5 %copy.79 = f32[1,128,3,128,3]{3,1,4,2,0:T(8,128)} copy(f32[1,128,3,128,3]{4,3,2,1,0:T(8,128)} %stack.94) | data formatting | bytes 1179648 | tf_op jit(solution)/shard_map/stack | solution.py:79
  146.8 3.8 %fusion.39 = (f32[384,384]{1,0:T(8,128)S(1)}, f32[384,384]{1,0:T(8,128)S(1)}) fusion(f32[385,384]{1,0:T(8,128)} %get-tuple-element.6, f32[384,385]{1,0:T(8,128)} %get-tuple-element.4, f32[386,386]{1,0:T(8,128)S(1)} %get-tuple-element.19, f32[384,385]{1,0:T(8,128)} %get-tuple-element.30, f32[385,384]{1,0:T(8,128)} %get-tuple-element.26, ...), kind=kLoop, calls=%fused_computation.81 | loop fusion | flops 2506752 | bytes 8257536 | tf_op jit(solution)/shard_map/sub | solution.py:72
  150.7 25.2 %stack.93 = f32[1,128,3,128,3]{4,3,2,1,0:T(8,128)} reshape(f32[384,384]{1,0:T(8,128)S(1)} %get-tuple-element.29) | data formatting | bytes 1179648 | tf_op jit(solution)/shard_map/stack | solution.py:79
  175.9 14.8 %copy.78 = f32[1,128,3,128,3]{3,1,4,2,0:T(8,128)S(1)} copy(f32[1,128,3,128,3]{4,3,2,1,0:T(8,128)} %stack.93) | data formatting | bytes 1179648 | tf_op jit(solution)/shard_map/stack | solution.py:79
  190.6 25.2 %stack.92 = f32[1,128,3,128,3]{4,3,2,1,0:T(8,128)} reshape(f32[384,384]{1,0:T(8,128)S(1)} %get-tuple-element.28) | data formatting | bytes 1179648 | tf_op jit(solution)/shard_map/stack | solution.py:79
  215.8 15.5 %copy.77 = f32[1,128,3,128,3]{3,1,4,2,0:T(8,128)} copy(f32[1,128,3,128,3]{4,3,2,1,0:T(8,128)} %stack.92) | data formatting | bytes 1179648 | tf_op jit(solution)/shard_map/stack | solution.py:79
  231.4 1.2 maximum_reduce_fusion
  232.7 3.3 %dynamic_update_slice.3 = f32[4,256,256]{2,1,0:T(8,128)S(1)} dynamic-update-slice(f32[4,256,256]{2,1,0:T(8,128)S(1)} %broadcast_in_dim.46, f32[4,128,128]{2,1,0:T(8,128)S(1)} %concatenate.16, s32[]{:T(128)} %constant.5.clone.1, s32[]{:T(128)S(6)} %select_n.21, s32[]{:T(128)S(6)} %select_n.22) | dynamic-update-slice | bytes 524292 | tf_op jit(solution)/shard_map/dynamic_update_slice | solution.py:132
  236.0 2.5 collective-permute-start.4
  238.5 10.6 %collective-permute-done.4 = f32[4,256,128]{2,1,0:T(8,128)S(1)} collective-permute-done((f32[4,256,128]{2,1,0:T(8,128)S(1)}, f32[4,256,128]{2,1,0:T(8,128)S(1)}, u32[]{:S(2)}, u32[]{:S(2)}) %collective-permute-start.4) | collective-permute-done | bytes 524320 | tf_op jit(solution)/shard_map/ppermute | solution.py:30
  249.3 2.5 collective-permute-start.5
  251.8 1.3 maximum_bitcast_fusion
  253.1 5.3 %collective-permute-done.5 = f32[4,128,128]{2,1,0:T(8,128)S(1)} collective-permute-done((f32[4,128,128]{2,1,0:T(8,128)S(1)}, f32[4,128,128]{2,1,0:T(8,128)S(1)}, u32[]{:S(2)}, u32[]{:S(2)}) %collective-permute-start.5) | collective-permute-done | bytes 262176 | tf_op jit(solution)/shard_map/ppermute | solution.py:30
  258.5 0.7 fusion.42
  (49 shorter events, 6.4 us)
Async XLA Ops:
  0.6 66.0 %copy-start = (s32[2,2]{1,0:T(2,128)S(1)}, s32[2,2]{1,0:T(2,128)}, u32[]{:S(2)}) copy-start(s32[2,2]{1,0:T(2,128)} %param.7) | copy-start | bytes 52
  13.1 7.3 %copy-start.4 = (s32[1,128,128]{2,1,0:T(8,128)S(1)}, s32[1,128,128]{2,1,0:T(8,128)}, u32[]{:S(2)}) copy-start(s32[1,128,128]{2,1,0:T(8,128)} %param.8) | copy-start | bytes 196612
  13.1 46.1 %all-to-all-start = ((f32[16,3,1,24,384]{4,3,1,2,0:T(8,128)}), f32[16,3,1,24,384]{4,3,1,2,0:T(8,128)}, u32[]{:S(2)}, u32[]{:S(2)}) async-start(f32[16,3,1,24,384]{4,3,1,2,0:T(8,128)} %fusion.43), calls=%async_computation | async-start | bytes 3538944 | tf_op jit(solution)/shard_map/all_to_all | solution.py:111
  20.7 0.8 copy-start.5
  20.7 0.8 copy-start.6
  60.8 5.9 %collective-permute-start.1 = (f32[5,1,384]{2,1,0:T(1,128)S(1)}, f32[5,1,384]{2,1,0:T(1,128)S(1)}, u32[]{:S(2)}, u32[]{:S(2)}) collective-permute-start(f32[5,1,384]{2,1,0:T(1,128)S(1)} %get-tuple-element.23), channel_id=1, source_target_pairs={{4,0},{8,4},{12,8},{5,1},{9,5},{13,9},{6,2},{10,6},{14,10},{7,3},{... | collective-permute-start | bytes 23048 | tf_op jit(solution)/shard_map/ppermute | solution.py:20
  63.9 6.4 %collective-permute-start = (f32[5,1,384]{2,1,0:T(1,128)S(1)}, f32[5,1,384]{2,1,0:T(1,128)S(1)}, u32[]{:S(2)}, u32[]{:S(2)}) collective-permute-start(f32[5,1,384]{2,1,0:T(1,128)S(1)} %get-tuple-element.22), channel_id=1, source_target_pairs={{0,4},{4,8},{8,12},{1,5},{5,9},{9,13},{2,6},{6,10},{10,14},{3,7},{... | collective-permute-start | bytes 23048 | tf_op jit(solution)/shard_map/ppermute | solution.py:18
  73.5 12.9 %collective-permute-start.3 = (f32[5,386,1]{1,2,0:T(1,128)S(1)}, f32[5,386,1]{1,2,0:T(1,128)S(1)}, u32[]{:S(2)}, u32[]{:S(2)}) collective-permute-start(f32[5,386,1]{1,2,0:T(1,128)S(1)} %copy.74), channel_id=1, source_target_pairs={{1,0},{2,1},{3,2},{5,4},{6,5},{7,6},{9,8},{10,9},{11,10},{13,12},{... | collective-permute-start | bytes 23168 | tf_op jit(solution)/shard_map/ppermute | solution.py:20
  79.9 7.9 %collective-permute-start.2 = (f32[5,386,1]{1,2,0:T(1,128)S(1)}, f32[5,386,1]{1,2,0:T(1,128)S(1)}, u32[]{:S(2)}, u32[]{:S(2)}) collective-permute-start(f32[5,386,1]{1,2,0:T(1,128)S(1)} %copy.73), channel_id=1, source_target_pairs={{0,1},{1,2},{2,3},{4,5},{5,6},{6,7},{8,9},{9,10},{10,11},{12,13},{... | collective-permute-start | bytes 23168 | tf_op jit(solution)/shard_map/ppermute | solution.py:18
  215.8 15.5 %copy-start.2 = (f32[1,128,3,128,3]{3,1,4,2,0:T(8,128)S(1)}, f32[1,128,3,128,3]{3,1,4,2,0:T(8,128)}, u32[]{:S(2)}) copy-start(f32[1,128,3,128,3]{3,1,4,2,0:T(8,128)} %copy.79) | copy-start | bytes 1769476
  236.0 13.1 %collective-permute-start.4 = (f32[4,256,128]{2,1,0:T(8,128)S(1)}, f32[4,256,128]{2,1,0:T(8,128)S(1)}, u32[]{:S(2)}, u32[]{:S(2)}) collective-permute-start(f32[4,256,128]{2,1,0:T(8,128)S(1)} %slice.343), channel_id=1, source_target_pairs={{0,1},{1,2},{2,3},{4,5},{5,6},{6,7},{8,9},{9,10},{10,11},{12,13},{... | collective-permute-start | bytes 1572872 | tf_op jit(solution)/shard_map/ppermute | solution.py:30
  249.3 9.2 %collective-permute-start.5 = (f32[4,128,128]{2,1,0:T(8,128)S(1)}, f32[4,128,128]{2,1,0:T(8,128)S(1)}, u32[]{:S(2)}, u32[]{:S(2)}) collective-permute-start(f32[4,128,128]{2,1,0:T(8,128)S(1)} %slice.345), channel_id=1, source_target_pairs={{0,4},{4,8},{8,12},{12,16},{16,20},{20,24},{24,28},{1,5},{5,9},{9,... | collective-permute-start | bytes 786440 | tf_op jit(solution)/shard_map/ppermute | solution.py:30
  251.7 7.5 %copy-start.1 = (s32[2,2]{1,0:T(2,128)S(1)}, s32[2,2]{1,0:T(2,128)}, u32[]{:S(2)}) copy-start(s32[2,2]{1,0:T(2,128)} %param.7) | copy-start | bytes 52
  251.7 6.7 %copy-start.3 = (f32[3,128,128]{2,1,0:T(8,128)S(1)}, f32[3,128,128]{2,1,0:T(8,128)}, u32[]{:S(2)}) copy-start(f32[3,128,128]{2,1,0:T(8,128)} %param.11) | copy-start | bytes 589828
